TPU v7x, 32 devices: a whole 2x2x4 slice. The times are simulated.
32 devices in a mesh: narrow: 4 (over x, core), wide: 8 (over z, y).
Axes of the slice: x: 2, y: 2, z: 4, core: 2. Of those that a mesh axis runs over, the one named last changes fastest.
Arguments:
- block_ids: int32 [512, 4], P(('narrow', 'wide')), may hold values from 0 to 511, as said below
- incidence: int32 [512, 4, 128, 128], P(('narrow', 'wide')), may hold values from 0 to 1
- costs: int32 [512, 128], P(('narrow', 'wide')), may hold values from 16 to 80
- start_mult: float32 [512, 128], replicated, may hold values from 0.25 to 4
- upper: float32 [1], replicated, may hold values from 65536 to 131072
Outputs:
- multipliers: float32 [512, 128], replicated
- primal_mean: float32 [512, 128], P(('narrow', 'wide'))
Inputs may be any that keep to these rules, and one draw needn't show every extreme that they name: `block_ids`: the 4 row blocks listed for one tile are distinct.
All inputs are finite; a program needn't handle non-finite values.
Results may differ from a plain program's by a relative error of at most 0.0003.
Values sent between devices are 32-bit elements; how exact they have to be, the bound alone decides.
A program may use at most 64 MiB of HBM per device.

v0:
```python
import jax
import jax.numpy as jnp
from jax import lax
from jax.sharding import PartitionSpec as P

BLK = 128
K = 4
ITERS = 3


def local(block_ids, incidence, costs, start_mult, upper):
    hi = lax.Precision.HIGHEST
    tiles_here = block_ids.shape[0]
    blocks = start_mult.shape[0]
    incf = incidence.astype(jnp.float32)
    costf = costs.astype(jnp.float32)
    onehot = (
        block_ids.reshape(tiles_here * K, 1) == jnp.arange(blocks, dtype=jnp.int32)[None, :]
    ).astype(jnp.float32)
    count_narrow = lax.axis_size("narrow")
    count_wide = lax.axis_size("wide")
    share_rows = blocks // lax.axis_size(("narrow", "wide"))
    share_start = lax.axis_index(("narrow", "wide")) * share_rows
    mult = start_mult
    primal_mean = jnp.zeros(costs.shape, jnp.float32)
    for step in range(ITERS):
        u_tile = jnp.take(mult, block_ids, axis=0)
        reduced = costf - jnp.einsum("tkrc,tkr->tc", incf, u_tile, precision=hi)
        primal = 1.0 / (1.0 + jnp.exp(reduced / 8.0))
        local_soft = jnp.sum(-8.0 * jax.nn.softplus(-reduced / 8.0))
        if step == 0:
            primal_mean = primal
        else:
            primal_mean = 0.3 * primal + 0.7 * primal_mean
        part = jnp.einsum("tkrc,tc->tkr", incf, primal_mean, precision=hi).reshape(
            tiles_here * K, BLK
        )
        row_part = jnp.dot(onehot.T, part, precision=hi, preferred_element_type=jnp.float32)
        outgoing = row_part.reshape(count_narrow, count_wide, share_rows, BLK)
        incoming = lax.all_to_all(
            lax.all_to_all(outgoing, "narrow", split_axis=0, concat_axis=0, tiled=True),
            "wide",
            split_axis=1,
            concat_axis=1,
            tiled=True,
        )
        cover_share = jnp.sum(jnp.sum(incoming, axis=0), axis=0)
        mult_share = lax.dynamic_slice_in_dim(mult, share_start, share_rows, 0)
        slope = 1.0 - cover_share
        norm, mult_total, late_sum = lax.psum(
            (jnp.sum(slope * slope), jnp.sum(mult_share), local_soft), ("narrow", "wide")
        )
        value = mult_total + late_sum
        size = (upper[0] - value) / (norm + 1e-06)
        new_share = jnp.maximum(0.0, mult_share + size * slope)
        mult = lax.all_gather(new_share, ("narrow", "wide"), axis=0, tiled=True)
    return (mult, primal_mean)


def solution(mesh):
    in_specs = (
        P(("narrow", "wide"), None),
        P(("narrow", "wide"), None, None, None),
        P(("narrow", "wide"), None),
        P(),
        P(),
    )
    out_specs = (P(), P(("narrow", "wide"), None))
    return jax.shard_map(local, mesh=mesh, in_specs=in_specs, out_specs=out_specs, check_vma=False)
```

profile of v0, /device:TPU:0, one launch (start us, length us, event | category | flops | bytes accessed | tf_op | source)
XLA Modules:
  0.0 426.2 jit_solution(1178383881923371404)
XLA Ops:
  0.6 0.7 compare_and_fusion
  1.3 0.7 compare_select_fusion.3
  2.0 0.8 copy.23
  3.2 1.5 gather_fusion
  4.8 4.1 fusion.10
  9.6 3.4 fusion.8
  13.3 10.0 %all_to_all.30 = f32[4,8,16,128]{3,2,1,0:T(8,128)S(1)} all-to-all(f32[4,8,16,128]{3,2,1,0:T(8,128)S(1)} %fusion.16), channel_id=1, replica_groups=mesh['narrow'=4,'wide'=8] {'narrow'}, dimensions={0} | all-to-all | bytes 524288 | tf_op jit(solution)/shard_map/all_to_all | solution.py:41
  23.3 0.7 copy.24
  24.1 5.8 %all-to-all-start.1 = ((f32[4,8,16,128]{3,2,0,1:T(8,128)}), f32[4,8,16,128]{3,2,0,1:T(8,128)S(1)}, u32[]{:S(2)}, u32[]{:S(2)}) async-start(f32[4,8,16,128]{3,2,0,1:T(8,128)} %copy.24), calls=%async_computation.1 | async-start | bytes 524288 | tf_op jit(solution)/shard_map/all_to_all | solution.py:40
  29.9 1.4 dynamic-slice_reduce_fusion.2
  32.6 5.8 %all-to-all-done.1 = f32[4,8,16,128]{3,2,0,1:T(8,128)S(1)} async-done(((f32[4,8,16,128]{3,2,0,1:T(8,128)}), f32[4,8,16,128]{3,2,0,1:T(8,128)S(1)}, u32[]{:S(2)}, u32[]{:S(2)}) %all-to-all-start.1) | async-done | bytes 262176 | tf_op jit(solution)/shard_map/all_to_all | solution.py:40
  39.7 39.0 %all-reduce.2 = (f32[]{:T(128)}, f32[]{:T(128)}) all-reduce(f32[]{:T(128)S(6)} %add.95, f32[]{:T(128)} %multiply_reduce_fusion.2), channel_id=1, replica_groups=mesh['narrow'=4,'wide'=8] {'narrow','wide'}, use_global_device_ids=true, to_apply=%region_1.2 | all-reduce | flops 2 | bytes 16 | tf_op jit(solution)/shard_map/psum | solution.py:50
  80.1 0.7 add_maximum_fusion.2
  80.8 67.3 %all_gather.9 = f32[512,128]{1,0:T(8,128)S(1)} all-gather(f32[16,128]{1,0:T(8,128)S(1)} %add_maximum_fusion.2), channel_id=1, replica_groups=mesh['narrow'=4,'wide'=8] {'narrow','wide'}, dimensions={0}, use_global_device_ids=true | all-gather | bytes 270336 | tf_op jit(solution)/shard_map/all_gather | solution.py:56
  148.8 4.1 fusion.6
  153.5 3.4 fusion.4
  157.3 8.4 %all_to_all.31 = f32[4,8,16,128]{3,2,1,0:T(8,128)S(1)} all-to-all(f32[4,8,16,128]{3,2,1,0:T(8,128)S(1)} %fusion.14), channel_id=1, replica_groups=mesh['narrow'=4,'wide'=8] {'narrow'}, dimensions={0} | all-to-all | bytes 524288 | tf_op jit(solution)/shard_map/all_to_all | solution.py:41
  165.7 0.7 copy.27
  166.4 3.4 all-to-all-start.3
  171.6 7.0 %all-to-all-done.3 = f32[4,8,16,128]{3,2,0,1:T(8,128)S(1)} async-done(((f32[4,8,16,128]{3,2,0,1:T(8,128)}), f32[4,8,16,128]{3,2,0,1:T(8,128)S(1)}, u32[]{:S(2)}, u32[]{:S(2)}) %all-to-all-start.3) | async-done | bytes 262176 | tf_op jit(solution)/shard_map/all_to_all | solution.py:40
  179.2 38.9 %all-reduce.1 = (f32[]{:T(128)}, f32[]{:T(128)}) all-reduce(f32[]{:T(128)S(6)} %add.100, f32[]{:T(128)} %multiply_reduce_fusion.1), channel_id=1, replica_groups=mesh['narrow'=4,'wide'=8] {'narrow','wide'}, use_global_device_ids=true, to_apply=%region_8.10 | all-reduce | flops 2 | bytes 16 | tf_op jit(solution)/shard_map/psum | solution.py:50
  219.5 67.5 %all_gather.10 = f32[512,128]{1,0:T(8,128)S(1)} all-gather(f32[16,128]{1,0:T(8,128)S(1)} %add_maximum_fusion.1), channel_id=1, replica_groups=mesh['narrow'=4,'wide'=8] {'narrow','wide'}, dimensions={0}, use_global_device_ids=true | all-gather | bytes 270336 | tf_op jit(solution)/shard_map/all_gather | solution.py:56
  287.6 4.1 fusion.2
  292.4 3.4 fusion
  296.1 8.4 %all_to_all.32 = f32[4,8,16,128]{3,2,1,0:T(8,128)S(1)} all-to-all(f32[4,8,16,128]{3,2,1,0:T(8,128)S(1)} %fusion.12), channel_id=1, replica_groups=mesh['narrow'=4,'wide'=8] {'narrow'}, dimensions={0} | all-to-all | bytes 524288 | tf_op jit(solution)/shard_map/all_to_all | solution.py:41
  304.5 0.7 copy.30
  305.2 3.4 all-to-all-start.5
  308.7 0.6 dynamic-slice_reduce_fusion
  310.5 6.9 %all-to-all-done.5 = f32[4,8,16,128]{3,2,0,1:T(8,128)S(1)} async-done(((f32[4,8,16,128]{3,2,0,1:T(8,128)}), f32[4,8,16,128]{3,2,0,1:T(8,128)S(1)}, u32[]{:S(2)}, u32[]{:S(2)}) %all-to-all-start.5) | async-done | bytes 262176 | tf_op jit(solution)/shard_map/all_to_all | solution.py:40
  318.1 38.9 %all-reduce = (f32[]{:T(128)}, f32[]{:T(128)}) all-reduce(f32[]{:T(128)S(6)} %add.106, f32[]{:T(128)} %multiply_reduce_fusion), channel_id=1, replica_groups=mesh['narrow'=4,'wide'=8] {'narrow','wide'}, use_global_device_ids=true, to_apply=%region_15.17 | all-reduce | flops 2 | bytes 16 | tf_op jit(solution)/shard_map/psum | solution.py:50
  358.2 67.3 %all_gather.11 = f32[512,128]{1,0:T(8,128)S(1)} all-gather(f32[16,128]{1,0:T(8,128)S(1)} %add_maximum_fusion), channel_id=1, replica_groups=mesh['narrow'=4,'wide'=8] {'narrow','wide'}, dimensions={0}, use_global_device_ids=true | all-gather | bytes 270336 | tf_op jit(solution)/shard_map/all_gather | solution.py:56
  425.5 0.7 copy.48
  (36 shorter events, 7.3 us)
Async XLA Ops:
  0.6 8.3 %copy-start.3 = (s32[16,128]{1,0:T(8,128)S(1)}, s32[16,128]{1,0:T(8,128)}, u32[]{:S(2)}) copy-start(s32[16,128]{1,0:T(8,128)} %param.9) | copy-start | bytes 24580
  4.7 4.9 %copy-start = (s32[16,4,128,128]{3,2,1,0:T(8,128)S(1)}, s32[16,4,128,128]{3,2,1,0:T(8,128)}, u32[]{:S(2)}) copy-start(s32[16,4,128,128]{3,2,1,0:T(8,128)} %param.8) | copy-start | bytes 12582916
  24.1 14.4 %all-to-all-start.1 = ((f32[4,8,16,128]{3,2,0,1:T(8,128)}), f32[4,8,16,128]{3,2,0,1:T(8,128)S(1)}, u32[]{:S(2)}, u32[]{:S(2)}) async-start(f32[4,8,16,128]{3,2,0,1:T(8,128)} %copy.24), calls=%async_computation.1 | async-start | bytes 524288 | tf_op jit(solution)/shard_map/all_to_all | solution.py:40
  148.7 4.8 %copy-start.1 = (s32[16,4,128,128]{3,2,1,0:T(8,128)S(1)}, s32[16,4,128,128]{3,2,1,0:T(8,128)}, u32[]{:S(2)}) copy-start(s32[16,4,128,128]{3,2,1,0:T(8,128)} %param.8) | copy-start | bytes 12582916
  166.4 12.2 %all-to-all-start.3 = ((f32[4,8,16,128]{3,2,0,1:T(8,128)}), f32[4,8,16,128]{3,2,0,1:T(8,128)S(1)}, u32[]{:S(2)}, u32[]{:S(2)}) async-start(f32[4,8,16,128]{3,2,0,1:T(8,128)} %copy.27), calls=%async_computation.3 | async-start | bytes 524288 | tf_op jit(solution)/shard_map/all_to_all | solution.py:40
  287.5 4.8 %copy-start.2 = (s32[16,4,128,128]{3,2,1,0:T(8,128)S(1)}, s32[16,4,128,128]{3,2,1,0:T(8,128)}, u32[]{:S(2)}) copy-start(s32[16,4,128,128]{3,2,1,0:T(8,128)} %param.8) | copy-start | bytes 12582916
  292.4 133.9 %copy-start.4 = (f32[16,128]{1,0:T(8,128)}, f32[16,128]{1,0:T(8,128)S(1)}, u32[]{:S(2)}) copy-start(f32[16,128]{1,0:T(8,128)S(1)} %get-tuple-element.18) | copy-start | bytes 24580
  305.2 12.2 %all-to-all-start.5 = ((f32[4,8,16,128]{3,2,0,1:T(8,128)}), f32[4,8,16,128]{3,2,0,1:T(8,128)S(1)}, u32[]{:S(2)}, u32[]{:S(2)}) async-start(f32[4,8,16,128]{3,2,0,1:T(8,128)} %copy.30), calls=%async_computation.5 | async-start | bytes 524288 | tf_op jit(solution)/shard_map/all_to_all | solution.py:40
where the time goes:
time: 427 us; the launch traced here: 426 us
  blocking collectives  346 us (81%)
  matrix products  23.5 us (6%)
  waiting for transfers between devices  19.7 us (5%)
  starting transfers between devices  12.7 us (3%)
  between operations  9.14 us (2%)
  other arithmetic  8.77 us (2%)
  local copies, waits for them, and re-layouts  6.74 us (2%)
    all_gather x3, blocking collectives, local(): mult = lax.all_gather(new_share, ('narrow', 'wide'), axis=0, tiled=True)  202 us
    psum x3, blocking collectives, local(): lax.psum((jnp.sum(slope * slope), jnp.sum(mult_share), local_soft), ('nar...  117 us
    all_to_all x3, blocking collectives, local(): lax.all_to_all(outgoing, 'narrow', split_axis=0, concat_axis=0, tiled=True)  26.8 us
    all_to_all x3, waiting for transfers between devices, local(): lax.all_to_all(lax.all_to_all(outgoing, 'narrow', split_axis=0, concat_ax...  19.7 us
    all_to_all x3, starting transfers between devices, local(): lax.all_to_all(lax.all_to_all(outgoing, 'narrow', split_axis=0, concat_ax...  12.7 us
    dot_general x3, matrix products, local(): reduced = costf - jnp.einsum('tkrc,tkr->tc', incf, u_tile, precision=hi)  12.3 us
    dot_general x3, matrix products, local(): jnp.einsum('tkrc,tc->tkr', incf, primal_mean, precision=hi)  10.2 us
  transfers between devices with their start and end apart: 3, of which 3 were waited for; matrix products, arithmetic and copies ran while one was open for 1% of the time, Pallas kernels for 0%

commit v1 on v0

--- a/solution.py
+++ b/solution.py
@@ -37,12 +37,20 @@
         )
         row_part = jnp.dot(onehot.T, part, precision=hi, preferred_element_type=jnp.float32)
         outgoing = row_part.reshape(count_narrow, count_wide, share_rows, BLK)
-        incoming = lax.all_to_all(
-            lax.all_to_all(outgoing, "narrow", split_axis=0, concat_axis=0, tiled=True),
-            "wide",
-            split_axis=1,
-            concat_axis=1,
-            tiled=True,
+        incoming = jnp.concatenate(
+            lax.all_to_all(
+                jnp.stack(
+                    jnp.split(
+                        lax.all_to_all(outgoing, "narrow", split_axis=0, concat_axis=0, tiled=True),
+                        lax.axis_size("wide"),
+                        axis=1,
+                    )
+                ),
+                "wide",
+                0,
+                0,
+            ),
+            axis=1,
         )
         cover_share = jnp.sum(jnp.sum(incoming, axis=0), axis=0)
         mult_share = lax.dynamic_slice_in_dim(mult, share_start, share_rows, 0)

time: 427 us -> 440 us (1.030)
  local copies, waits for them, and re-layouts: 6.74 us -> 19.4 us
    unnamed x12 -> x33, local copies, waits for them, and re-layouts: 1.48 us -> 14.4 us
where the time goes in v1:
time: 440 us; the launch traced here: 439 us
  blocking collectives  346 us (79%)
  matrix products  23.5 us (5%)
  waiting for transfers between devices  19.7 us (4%)
  local copies, waits for them, and re-layouts  19.4 us (4%)
  starting transfers between devices  12.7 us (3%)
  between operations  9.15 us (2%)
  other arithmetic  8.77 us (2%)
    all_gather x3, blocking collectives, local(): mult = lax.all_gather(new_share, ('narrow', 'wide'), axis=0, tiled=True)  202 us
    psum x3, blocking collectives, local(): lax.psum((jnp.sum(slope * slope), jnp.sum(mult_share), local_soft), ('nar...  117 us
    all_to_all x3, blocking collectives, local(): lax.all_to_all(outgoing, 'narrow', split_axis=0, concat_axis=0, tiled=True)  26.8 us
    all_to_all x3, waiting for transfers between devices, local(): lax.all_to_all(jnp.stack(jnp.split(lax.all_to_all(outgoing, 'narrow', spl...  19.7 us
    unnamed x33, local copies, waits for them, and re-layouts  14.4 us
    all_to_all x3, starting transfers between devices, local(): lax.all_to_all(jnp.stack(jnp.split(lax.all_to_all(outgoing, 'narrow', spl...  12.7 us
    dot_general x3, matrix products, local(): reduced = costf - jnp.einsum('tkrc,tkr->tc', incf, u_tile, precision=hi)  12.3 us
    dot_general x3, matrix products, local(): jnp.einsum('tkrc,tc->tkr', incf, primal_mean, precision=hi)  10.2 us
  transfers between devices with their start and end apart: 3, of which 3 were waited for; matrix products, arithmetic and copies ran while one was open for 1% of the time, Pallas kernels for 0%

profile of v1, /device:TPU:0, one launch (start us, length us, event | category | flops | bytes accessed | tf_op | source)
XLA Modules:
  0.0 438.9 jit_solution(5972429225273998544)
XLA Ops:
  0.6 0.7 compare_and_fusion
  1.3 0.7 compare_select_fusion.3
  2.0 0.8 copy.37
  3.2 1.5 gather_fusion
  4.8 4.1 fusion.10
  8.9 0.6 fusion.25
  9.6 3.4 fusion.8
  13.3 10.0 %all_to_all.30 = f32[4,8,16,128]{3,2,1,0:T(8,128)S(1)} all-to-all(f32[4,8,16,128]{3,2,1,0:T(8,128)S(1)} %fusion.16), channel_id=1, replica_groups=mesh['narrow'=4,'wide'=8] {'narrow'}, dimensions={0} | all-to-all | bytes 524288 | tf_op jit(solution)/shard_map/all_to_all | solution.py:44
  23.3 0.6 constant_dynamic-update-slice_fusion.7
  28.3 5.8 %all-to-all-start.1 = ((f32[8,4,1,16,128]{4,3,1,2,0:T(8,128)}), f32[8,4,1,16,128]{4,3,1,2,0:T(8,128)S(1)}, u32[]{:S(2)}, u32[]{:S(2)}) async-start(f32[8,4,1,16,128]{4,3,1,2,0:T(8,128)} %constant_dynamic-update-slice_fusion), calls=%async_computation.1 | async-start | bytes 524288 | tf_op jit(solution)/shard_map/all_to_all | solution.py:41
  34.1 1.4 dynamic-slice_reduce_fusion.2
  36.8 5.8 %all-to-all-done.1 = f32[8,4,1,16,128]{4,3,1,2,0:T(8,128)S(1)} async-done(((f32[8,4,1,16,128]{4,3,1,2,0:T(8,128)}), f32[8,4,1,16,128]{4,3,1,2,0:T(8,128)S(1)}, u32[]{:S(2)}, u32[]{:S(2)}) %all-to-all-start.1) | async-done | bytes 262176 | tf_op jit(solution)/shard_map/all_to_all | solution.py:41
  44.0 39.0 %all-reduce.2 = (f32[]{:T(128)}, f32[]{:T(128)}) all-reduce(f32[]{:T(128)S(6)} %add.95, f32[]{:T(128)} %multiply_reduce_fusion.2), channel_id=1, replica_groups=mesh['narrow'=4,'wide'=8] {'narrow','wide'}, use_global_device_ids=true, to_apply=%region_1.2 | all-reduce | flops 2 | bytes 16 | tf_op jit(solution)/shard_map/psum | solution.py:58
  84.3 0.7 add_maximum_fusion.2
  85.1 67.3 %all_gather.9 = f32[512,128]{1,0:T(8,128)S(1)} all-gather(f32[16,128]{1,0:T(8,128)S(1)} %add_maximum_fusion.2), channel_id=1, replica_groups=mesh['narrow'=4,'wide'=8] {'narrow','wide'}, dimensions={0}, use_global_device_ids=true | all-gather | bytes 270336 | tf_op jit(solution)/shard_map/all_gather | solution.py:64
  153.0 4.1 fusion.6
  157.1 0.6 fusion.27
  157.7 3.4 fusion.4
  161.5 8.4 %all_to_all.31 = f32[4,8,16,128]{3,2,1,0:T(8,128)S(1)} all-to-all(f32[4,8,16,128]{3,2,1,0:T(8,128)S(1)} %fusion.14), channel_id=1, replica_groups=mesh['narrow'=4,'wide'=8] {'narrow'}, dimensions={0} | all-to-all | bytes 524288 | tf_op jit(solution)/shard_map/all_to_all | solution.py:44
  174.8 3.4 all-to-all-start.3
  180.1 7.0 %all-to-all-done.3 = f32[8,4,1,16,128]{4,3,1,2,0:T(8,128)S(1)} async-done(((f32[8,4,1,16,128]{4,3,1,2,0:T(8,128)}), f32[8,4,1,16,128]{4,3,1,2,0:T(8,128)S(1)}, u32[]{:S(2)}, u32[]{:S(2)}) %all-to-all-start.3) | async-done | bytes 262176 | tf_op jit(solution)/shard_map/all_to_all | solution.py:41
  187.6 38.9 %all-reduce.1 = (f32[]{:T(128)}, f32[]{:T(128)}) all-reduce(f32[]{:T(128)S(6)} %add.100, f32[]{:T(128)} %multiply_reduce_fusion.1), channel_id=1, replica_groups=mesh['narrow'=4,'wide'=8] {'narrow','wide'}, use_global_device_ids=true, to_apply=%region_8.10 | all-reduce | flops 2 | bytes 16 | tf_op jit(solution)/shard_map/psum | solution.py:58
  227.9 67.5 %all_gather.10 = f32[512,128]{1,0:T(8,128)S(1)} all-gather(f32[16,128]{1,0:T(8,128)S(1)} %add_maximum_fusion.1), channel_id=1, replica_groups=mesh['narrow'=4,'wide'=8] {'narrow','wide'}, dimensions={0}, use_global_device_ids=true | all-gather | bytes 270336 | tf_op jit(solution)/shard_map/all_gather | solution.py:64
  296.1 4.1 fusion.2
  300.8 3.4 fusion
  304.5 8.4 %all_to_all.32 = f32[4,8,16,128]{3,2,1,0:T(8,128)S(1)} all-to-all(f32[4,8,16,128]{3,2,1,0:T(8,128)S(1)} %fusion.12), channel_id=1, replica_groups=mesh['narrow'=4,'wide'=8] {'narrow'}, dimensions={0} | all-to-all | bytes 524288 | tf_op jit(solution)/shard_map/all_to_all | solution.py:44
  317.9 3.4 all-to-all-start.5
  321.3 0.6 dynamic-slice_reduce_fusion
  323.1 6.9 %all-to-all-done.5 = f32[8,4,1,16,128]{4,3,1,2,0:T(8,128)S(1)} async-done(((f32[8,4,1,16,128]{4,3,1,2,0:T(8,128)}), f32[8,4,1,16,128]{4,3,1,2,0:T(8,128)S(1)}, u32[]{:S(2)}, u32[]{:S(2)}) %all-to-all-start.5) | async-done | bytes 262176 | tf_op jit(solution)/shard_map/all_to_all | solution.py:41
  330.7 38.9 %all-reduce = (f32[]{:T(128)}, f32[]{:T(128)}) all-reduce(f32[]{:T(128)S(6)} %add.106, f32[]{:T(128)} %multiply_reduce_fusion), channel_id=1, replica_groups=mesh['narrow'=4,'wide'=8] {'narrow','wide'}, use_global_device_ids=true, to_apply=%region_15.17 | all-reduce | flops 2 | bytes 16 | tf_op jit(solution)/shard_map/psum | solution.py:58
  370.9 67.3 %all_gather.11 = f32[512,128]{1,0:T(8,128)S(1)} all-gather(f32[16,128]{1,0:T(8,128)S(1)} %add_maximum_fusion), channel_id=1, replica_groups=mesh['narrow'=4,'wide'=8] {'narrow','wide'}, dimensions={0}, use_global_device_ids=true | all-gather | bytes 270336 | tf_op jit(solution)/shard_map/all_gather | solution.py:64
  438.2 0.7 copy.122
  (57 shorter events, 20.2 us)
Async XLA Ops:
  0.6 8.3 %copy-start.3 = (s32[16,128]{1,0:T(8,128)S(1)}, s32[16,128]{1,0:T(8,128)}, u32[]{:S(2)}) copy-start(s32[16,128]{1,0:T(8,128)} %param.9) | copy-start | bytes 24580
  4.7 4.9 %copy-start = (s32[16,4,128,128]{3,2,1,0:T(8,128)S(1)}, s32[16,4,128,128]{3,2,1,0:T(8,128)}, u32[]{:S(2)}) copy-start(s32[16,4,128,128]{3,2,1,0:T(8,128)} %param.8) | copy-start | bytes 12582916
  28.3 14.4 %all-to-all-start.1 = ((f32[8,4,1,16,128]{4,3,1,2,0:T(8,128)}), f32[8,4,1,16,128]{4,3,1,2,0:T(8,128)S(1)}, u32[]{:S(2)}, u32[]{:S(2)}) async-start(f32[8,4,1,16,128]{4,3,1,2,0:T(8,128)} %constant_dynamic-update-slice_fusion), calls=%async_computation.1 | async-start | bytes 524288 | tf_op jit(solution)/shard_map/all_to_all | solution.py:41
  152.9 4.8 %copy-start.1 = (s32[16,4,128,128]{3,2,1,0:T(8,128)S(1)}, s32[16,4,128,128]{3,2,1,0:T(8,128)}, u32[]{:S(2)}) copy-start(s32[16,4,128,128]{3,2,1,0:T(8,128)} %param.8) | copy-start | bytes 12582916
  174.8 12.2 %all-to-all-start.3 = ((f32[8,4,1,16,128]{4,3,1,2,0:T(8,128)}), f32[8,4,1,16,128]{4,3,1,2,0:T(8,128)S(1)}, u32[]{:S(2)}, u32[]{:S(2)}) async-start(f32[8,4,1,16,128]{4,3,1,2,0:T(8,128)} %constant_dynamic-update-slice_fusion.8), calls=%async_computation.3 | async-start | bytes 524288 | tf_op jit(solution)/shard_map/all_to_all | solution.py:41
  296.0 4.8 %copy-start.2 = (s32[16,4,128,128]{3,2,1,0:T(8,128)S(1)}, s32[16,4,128,128]{3,2,1,0:T(8,128)}, u32[]{:S(2)}) copy-start(s32[16,4,128,128]{3,2,1,0:T(8,128)} %param.8) | copy-start | bytes 12582916
  300.8 138.1 %copy-start.4 = (f32[16,128]{1,0:T(8,128)}, f32[16,128]{1,0:T(8,128)S(1)}, u32[]{:S(2)}) copy-start(f32[16,128]{1,0:T(8,128)S(1)} %get-tuple-element.18) | copy-start | bytes 24580
  317.9 12.2 %all-to-all-start.5 = ((f32[8,4,1,16,128]{4,3,1,2,0:T(8,128)}), f32[8,4,1,16,128]{4,3,1,2,0:T(8,128)S(1)}, u32[]{:S(2)}, u32[]{:S(2)}) async-start(f32[8,4,1,16,128]{4,3,1,2,0:T(8,128)} %constant_dynamic-update-slice_fusion.16), calls=%async_computation.5 | async-start | bytes 524288 | tf_op jit(solution)/shard_map/all_to_all | solution.py:41
